TPU v7x, 32 devices: a whole 2x2x4 slice. The times are simulated.
32 devices in a mesh: lat: 8 (over y, x, core), lon: 4 (over z).
Axes of the slice: x: 2, y: 2, z: 4, core: 2. Of those that a mesh axis runs over, the one named last changes fastest.
Arguments:
- current: bfloat16 [69, 256, 512], P(None, 'lat', 'lon')
- next_fields: bfloat16 [96, 256, 512], P(('lat', 'lon')), may hold values from -6 to 6
- reader_slot: int32 [69], replicated, may hold values from 0 to 95, as said below
- first_weight: bfloat16 [9, 256, 69], replicated, may hold values from -0.25 to 0.25
- first_bias: float32 [256], replicated, may hold values from -3 to 3
- second_weight: bfloat16 [9, 256, 256], replicated, may hold values from -0.125 to 0.125
- second_bias: float32 [256], replicated, may hold values from -3 to 3
Outputs:
- features: bfloat16 [256, 256, 512], P(None, 'lat', 'lon')
- next_tile: bfloat16 [69, 256, 512], P(None, 'lat', 'lon')
Inputs may be any that keep to these rules, and one draw needn't show every extreme that they name: `reader_slot`: the 69 entries are different slots.
All inputs are finite; a program needn't handle non-finite values.
Results may differ from a plain program's by a relative error of at most 0.0053.
Values may be sent and summed in bfloat16 or wider, within the bound.
A program may use at most 128 MiB of HBM per device.

v0:
```python
import functools

import jax
import jax.numpy as jnp
from jax import lax
from jax.experimental import pallas as pl
from jax.experimental.pallas import tpu as pltpu
from jax.sharding import PartitionSpec as P

MESH = pl.DeviceIdType.MESH
F32 = jnp.float32
BF16 = jnp.bfloat16
LANES = 128
G1 = 4
G2 = 8


def twice_half_gelu(u):
    return u + u * jnp.tanh(u * (1.5957691216057308 + 0.2854179950588114 * (u * u)))


def kernel(
    dims, cur_in, nf, w1_in, b1_in, w2_in, b2_in, feat, moved,
    cur, w1, w2, b1, b2, yf, xf, parts, turned, xs, cols, csend, hcol, rsend, rrecv, en, eh,
    xn, acc1, hp, hs, acc2, w1s, w2s, stats,
    in_sem, st_send, st_recv, ha_send, ha_recv, mv_send, mv_recv, own_sem,
):
    n_lat, n_lon, chans, rows, wide, slots, hid = dims
    n = n_lat * n_lon
    cp = -(-chans // 8) * 8
    kq = xs.shape[2]
    cb = rsend.shape[2]
    pitch = xf.shape[1]
    xflat = xf.reshape(cp * pitch, wide)
    yflat = yf.reshape(hid * pitch, wide)
    lat = lax.axis_index("lat")
    lon = lax.axis_index("lon")
    me = lat * n_lon + lon

    loads = [
        pltpu.make_async_copy(src, dst, in_sem.at[i])
        for i, (src, dst) in enumerate(((cur_in, cur), (w1_in, w1), (w2_in, w2), (b1_in, b1), (b2_in, b2)))
    ]
    for load in loads:
        load.start()

    barrier = pltpu.get_barrier_semaphore()

    def greet(d, carry):
        t = lax.rem(me + d, n)
        pl.semaphore_signal(
            barrier, inc=1, device_id=(t // n_lon, lax.rem(t, n_lon)), device_id_type=MESH
        )
        return carry

    lax.fori_loop(1, n, greet, 0)

    loads[0].wait()
    x = cur[...].astype(F32)
    xf[0:chans, 0:rows, :] = x
    by = x.reshape(chans, rows // 8, 8, wide)
    parts[0, 0 : chans * 8, :] = jnp.sum(by, axis=1).reshape(chans * 8, wide)
    parts[1, 0 : chans * 8, :] = jnp.sum(by * by, axis=1).reshape(chans * 8, wide)
    if cp > chans:
        xf[chans:cp, :, :] = jnp.zeros((cp - chans, pitch, wide), F32)
        for k in range(2):
            parts[k, chans * 8 : cp * 8, :] = jnp.zeros(((cp - chans) * 8, wide), F32)
    for k in range(2):
        s = parts[k, pl.ds(0, cp, stride=8), :]
        for j in range(1, 8):
            s = s + parts[k, pl.ds(j, cp, stride=8), :]
        s = jnp.concatenate([s, jnp.zeros((LANES - cp, wide), F32)], axis=0).T
        stats[pl.ds(me, 1), k : k + 1, :] = jnp.sum(s, axis=0, keepdims=True)[None]

    def raw_row(r):
        return xflat[pl.ds(r, cp, stride=pitch), :]

    for side, r in ((0, 0), (1, rows - 2)):
        for j in range(2):
            a = jnp.concatenate([raw_row(r + j), jnp.zeros((cb - cp, wide), F32)], axis=0)
            rsend[side, j] = a.astype(BF16)

    group = lax.broadcasted_iota(jnp.int32, (1, wide), 1) // 4
    per = wide // 4
    for base in range(0, rows, per):
        strip = jnp.zeros((cp, wide), F32)
        for r in range(min(per, rows - base)):
            strip = jnp.where(group == r, pltpu.roll(raw_row(base + r), 4 * r + 2, 1), strip)
        turned[...] = jnp.concatenate([strip, jnp.zeros((LANES - cp, wide), F32)], axis=0).T
        part = min(per, rows - base)
        e0, e1, w0, w1_ = [turned[pl.ds(c, part, stride=4), :][:, 0:cp] for c in range(4)]
        blank = jnp.zeros((part, kq - 3 * cp), F32)
        cols[0, base : base + part] = jnp.concatenate([e1, w0, w1_, blank], axis=1)
        cols[1, base : base + part] = jnp.concatenate([e0, e1, w0, blank], axis=1)
    for side in range(2):
        csend[side] = cols[side].astype(BF16)

    pl.semaphore_wait(barrier, n - 1)

    def stat_copy(d):
        t = lax.rem(me + d, n)
        return pltpu.make_async_remote_copy(
            src_ref=stats.at[me], dst_ref=stats.at[me],
            send_sem=st_send, recv_sem=st_recv,
            device_id=(t // n_lon, lax.rem(t, n_lon)), device_id_type=MESH,
        )

    def stat_start(d, carry):
        stat_copy(d).start()
        return carry


    lax.fori_loop(1, n, stat_start, 0)

    north, south = lax.rem(lat + n_lat - 1, n_lat), lax.rem(lat + 1, n_lat)
    west, east = lax.rem(lon + n_lon - 1, n_lon), lax.rem(lon + 1, n_lon)
    halos = [
        (rsend.at[0], rrecv.at[1], (north, lon)),
        (rsend.at[1], rrecv.at[0], (south, lon)),
    ]
    for side, col_to in ((0, west), (1, east)):
        into = 1 - side
        halos.append((csend.at[side], hcol.at[into, pl.ds(16, rows)], (lat, col_to)))
        halos.append((csend.at[side, pl.ds(0, 16)], hcol.at[into, pl.ds(16 + rows, 16)], (north, col_to)))
        halos.append((csend.at[side, pl.ds(rows - 16, 16)], hcol.at[into, pl.ds(0, 16)], (south, col_to)))
    copies = [
        pltpu.make_async_remote_copy(
            src_ref=src, dst_ref=dst, send_sem=ha_send.at[i], recv_sem=ha_recv.at[i],
            device_id=where, device_id_type=MESH,
        )
        for i, (src, dst, where) in enumerate(halos)
    ]
    for copy in copies:
        copy.start()


    half = max(n_lon // 2, 1)

    def field_start(i, carry):
        j = i // n_lat
        if n_lon % 2 == 0:
            mine = lon // half
            far = (1 - mine) * half + j
            near = mine * half + lax.rem(lax.rem(lon, half) + j - half + 1, half)
            tn = jnp.where(j < half, far, near)
        else:
            tn = lax.rem(lon + 1 + j, n_lon)
        k = lax.rem(i, n_lat) + jnp.where(j == n_lon - 1, 1, 0)
        tl = lax.rem(lat + k, n_lat)
        pltpu.make_async_remote_copy(
            src_ref=nf.at[:, pl.ds(pl.multiple_of(tl * rows, rows), rows), pl.ds(pl.multiple_of(tn * wide, wide), wide)],
            dst_ref=moved.at[pl.ds(me * slots, slots)],
            send_sem=mv_send, recv_sem=mv_recv,
            device_id=(tl, tn), device_id_type=MESH,
        ).start()
        return carry


    cuts = [min(e, n - 1) for e in (0, 0, 4, 8)] + [n - 1]
    lax.fori_loop(0, cuts[1], field_start, 0)
    own = pltpu.make_async_copy(
        nf.at[:, pl.ds(pl.multiple_of(lat * rows, rows), rows), pl.ds(pl.multiple_of(lon * wide, wide), wide)],
        moved.at[pl.ds(me * slots, slots)],
        own_sem,
    )
    own.start()

    def turn(a, p):
        lo = pltpu.roll(a, 1, 1)
        hi = pltpu.roll(a, wide - 1, 1)
        stacked = jnp.concatenate([lo, a, hi, jnp.zeros((kq - 3 * cp, wide), F32)], axis=0)
        xs[p] = stacked.astype(BF16).T

    def turn_row(r, carry):
        turn(raw_row(r), r + 2)
        return carry

    lax.fori_loop(0, rows, turn_row, 0, unroll=4)

    lax.fori_loop(cuts[1], cuts[2], field_start, 0)
    for load in loads[1:]:
        load.wait()
    for a in range(3):
        pieces = []
        for j in range(3):
            pieces.append(w1[3 * a + j].astype(F32))
            if cp > chans:
                pieces.append(jnp.zeros((cp - chans, hid), F32))
        pieces.append(jnp.zeros((kq - 3 * cp, hid), F32))
        w1s[pl.ds(a * kq, kq), :] = (0.5 * jnp.concatenate(pieces, axis=0)).astype(BF16)

    def turn_weight(tap, carry):
        w2s[pl.ds(pl.multiple_of(tap * hid, hid), hid), :] = w2[tap].T
        return carry

    lax.fori_loop(0, 9, turn_weight, 0)

    lax.fori_loop(cuts[2], cuts[3], field_start, 0)
    for copy in copies:
        copy.wait_recv()
    lax.fori_loop(cuts[3], cuts[4], field_start, 0)
    tall = rows + 4
    step = en.shape[1]
    for side, p in ((0, 0), (1, rows + 2)):
        for j in range(2):
            turn(rrecv[side, j].astype(F32)[0:cp], p + j)

    lane = lax.broadcasted_iota(jnp.int32, (1, kq), 1)
    for side in range(2):
        far = hcol[side].astype(F32)[14 : 14 + tall]
        mine = jnp.concatenate(
            [
                xs[p, (wide - 16 if side == 0 else 0) : (wide if side == 0 else 16), :].astype(F32)[(15 if side == 0 else 0) : (16 if side == 0 else 1)]
                for p in (0, 1)
            ]
            + [cols[1 - side]]
            + [
                xs[p, (wide - 16 if side == 0 else 0) : (wide if side == 0 else 16), :].astype(F32)[(15 if side == 0 else 0) : (16 if side == 0 else 1)]
                for p in (rows + 2, rows + 3)
            ],
            axis=0,
        )
        theirs = lane < 2 * cp if side == 0 else lane >= cp
        en[side, 0:tall, :] = jnp.where(theirs, far, mine)
        en[2 + side, 0:tall, :] = pltpu.roll(far, kq - cp if side == 0 else cp, 1)

    def patch(p, carry):
        first = xs[p, 0:16, :].astype(F32)
        spot = lax.broadcasted_iota(jnp.int32, (16, 1), 0)
        xs[p, 0:16, :] = jnp.where((spot == 0) & (lane < cp), en[2, pl.ds(p, 1), :], first).astype(BF16)
        last = xs[p, wide - 16 : wide, :].astype(F32)
        xs[p, wide - 16 : wide, :] = jnp.where(
            (spot == 15) & (lane >= 2 * cp) & (lane < 3 * cp), en[3, pl.ds(p, 1), :], last
        ).astype(BF16)
        return carry

    lax.fori_loop(0, tall, patch, 0)

    many = pltpu.make_async_copy(stats.at[pl.ds(0, n - 1)], stats.at[pl.ds(0, n - 1)], st_recv)
    many.wait()
    sums = jnp.sum(stats[...], axis=0)
    cells = n * rows * wide
    mean = sums[0:1] / cells
    scale = 1.0 / jnp.sqrt(sums[1:2] / cells - mean * mean + 1e-05)

    def thrice(v):
        v = v[:, 0:cp]
        return jnp.concatenate([v, v, v, jnp.zeros((1, kq - 3 * cp), F32)], axis=1)

    mean3 = thrice(mean)
    scale3 = thrice(scale)

    def normal(p, carry):
        xn[p] = ((xs[p].astype(F32) - mean3) * scale3).astype(BF16)
        return carry

    lax.fori_loop(0, tall, normal, 0, unroll=2)

    @pl.when(lat == 0)
    def _():
        xn[0:2] = jnp.zeros((2, wide, kq), BF16)

    @pl.when(lat == n_lat - 1)
    def _():
        xn[rows + 2 : rows + 4] = jnp.zeros((2, wide, kq), BF16)

    first = jnp.where(lat == 0, 0, -2)
    last = jnp.where(lat == n_lat - 1, rows - 1, rows + 1)
    line = lax.broadcasted_iota(jnp.int32, (step, 1), 0) - 2
    inside = (line >= first) & (line <= last)
    bias1 = 0.5 * b1[...]
    bias2 = b2[...]
    edge = jnp.concatenate(
        [jnp.where(inside, (en[side] - mean3) * scale3, 0.0) for side in range(2)], axis=0
    ).astype(BF16)
    z = [jnp.dot(edge, w1s[pl.ds(a * kq, kq), :], preferred_element_type=F32) for a in range(3)]
    for side in range(2):
        at = side * step
        h = z[0][at : at + rows + 2] + z[1][at + 1 : at + rows + 3] + z[2][at + 2 : at + rows + 4] + bias1
        eh[side, pl.ds(0, rows + 2), :] = twice_half_gelu(h)

    def conv1(q, g):
        left = jnp.concatenate([xn[pl.ds(q + a, g)].reshape(g * wide, kq) for a in range(3)], axis=1)
        acc1[0 : g * wide] = jnp.dot(left, w1s[...], preferred_element_type=F32)

    def store1(q, g):
        for k in range(g):
            hp[k, 8 : 8 + wide, :] = twice_half_gelu(acc1[k * wide : (k + 1) * wide, :] + bias1)
            hp[k, 7:8, :] = eh[0, pl.ds(q + k, 1), :]
            hp[k, 8 + wide : 9 + wide, :] = eh[1, pl.ds(q + k, 1), :]
            for m in range(3):
                hs[q + k, :, m * hid : (m + 1) * hid] = hp[k, 7 + m : 7 + m + wide, :].astype(BF16)

    def phase1(b, carry):
        store1(G1 * (b - 1), G1)
        conv1(G1 * b, G1)
        return carry

    conv1(0, G1)
    whole1 = (rows + 2) // G1
    lax.fori_loop(1, whole1, phase1, 0)
    store1(G1 * (whole1 - 1), G1)
    if (rows + 2) % G1:
        conv1(G1 * whole1, (rows + 2) % G1)
        store1(G1 * whole1, (rows + 2) % G1)

    @pl.when(lat == 0)
    def _():
        hs[0] = jnp.zeros((wide, 3 * hid), BF16)

    @pl.when(lat == n_lat - 1)
    def _():
        hs[rows + 1] = jnp.zeros((wide, 3 * hid), BF16)

    def conv2(q):
        left = jnp.concatenate([hs[pl.ds(q + a, G2)].reshape(G2 * wide, 3 * hid) for a in range(3)], axis=1)
        acc2[...] = jnp.dot(left, w2s[...], preferred_element_type=F32)

    def store2(q):
        for k in range(G2):
            yflat[pl.ds(q + k, hid, stride=pitch), :] = (acc2[k * wide : (k + 1) * wide, :] + bias2).T

    def phase2(b, carry):
        store2(G2 * (b - 1))
        conv2(G2 * b)
        return carry

    conv2(0)
    lax.fori_loop(1, rows // G2, phase2, 0)
    store2(rows - G2)

    chunk = hid // 8
    for k in range(8):
        part = pl.ds(k * chunk, chunk)
        feat[part] = yf[part, 0:rows, :].astype(BF16)

    own.wait()
    others = moved.at[pl.ds(0, (n - 1) * slots)]
    pltpu.make_async_copy(others, others, mv_recv).wait()
    pltpu.make_async_copy(others, others, mv_send).wait()
    pltpu.make_async_copy(stats.at[pl.ds(0, n - 1)], stats.at[pl.ds(0, n - 1)], st_send).wait()
    for copy in copies:
        copy.wait_send()


def give(chans, feat_in, moved, slot_in, feat, tile, slot, sems):
    want = pltpu.make_async_copy(slot_in, slot, sems.at[0])
    want.start()
    out = pltpu.make_async_copy(feat_in, feat, sems.at[1])
    out.start()
    want.wait()

    def take(c, carry):
        pltpu.make_async_copy(moved.at[slot[c]], tile.at[c], sems.at[2]).start()
        return carry

    lax.fori_loop(0, chans, take, 0)
    pltpu.make_async_copy(moved.at[pl.ds(0, chans)], tile, sems.at[2]).wait()
    out.wait()


def body(current, next_fields, reader_slot, first_weight, first_bias, second_weight, second_bias):
    n_lat, n_lon = lax.axis_size("lat"), lax.axis_size("lon")
    n = n_lat * n_lon
    chans, rows, wide = current.shape
    slots = next_fields.shape[0]
    hid = first_weight.shape[1]
    cp = -(-chans // 8) * 8
    cb = -(-chans // 16) * 16
    kq = -(-3 * cp // LANES) * LANES
    pitch = 8 * (rows // 8 + 1 - rows // 8 % 2)
    step = -(-(rows + 4) // 16) * 16
    dims = (n_lat, n_lon, chans, rows, wide, slots, hid)
    vmem = pl.BlockSpec(memory_space=pltpu.VMEM)
    hbm = pl.BlockSpec(memory_space=pltpu.HBM)
    hold = pltpu.with_memory_space_constraint
    made, moved = pl.pallas_call(
        functools.partial(kernel, dims),
        out_shape=(
            jax.ShapeDtypeStruct((hid, rows, wide), BF16),
            jax.ShapeDtypeStruct((n * slots, rows, wide), BF16),
        ),
        in_specs=[hbm] * 6,
        out_specs=(vmem, vmem),
        scratch_shapes=[
            pltpu.VMEM((chans, rows, wide), BF16),
            pltpu.VMEM((9, chans, hid), BF16),
            pltpu.VMEM((9, hid, hid), BF16),
            pltpu.VMEM((1, hid), F32),
            pltpu.VMEM((1, hid), F32),
            pltpu.VMEM((hid, pitch, wide), F32),
            pltpu.VMEM((cp, pitch, wide), F32),
            pltpu.VMEM((2, cp * 8, wide), F32),
            pltpu.VMEM((wide, LANES), F32),
            pltpu.VMEM((rows + 4, wide, kq), BF16),
            pltpu.VMEM((2, rows, kq), F32),
            pltpu.VMEM((2, rows, kq), BF16),
            pltpu.VMEM((2, rows + 32, kq), BF16),
            pltpu.VMEM((2, 2, cb, wide), BF16),
            pltpu.VMEM((2, 2, cb, wide), BF16),
            pltpu.VMEM((4, step, kq), F32),
            pltpu.VMEM((2, step, hid), F32),
            pltpu.VMEM((rows + 4, wide, kq), BF16),
            pltpu.VMEM((G1 * wide, hid), F32),
            pltpu.VMEM((G1, wide + 16, hid), F32),
            pltpu.VMEM((rows + 2, wide, 3 * hid), BF16),
            pltpu.VMEM((G2 * wide, hid), F32),
            pltpu.VMEM((3 * kq, hid), BF16),
            pltpu.VMEM((9 * hid, hid), BF16),
            pltpu.VMEM((n, 2, LANES), F32),
            pltpu.SemaphoreType.DMA((5,)),
            pltpu.SemaphoreType.DMA,
            pltpu.SemaphoreType.DMA,
            pltpu.SemaphoreType.DMA((8,)),
            pltpu.SemaphoreType.DMA((8,)),
            pltpu.SemaphoreType.DMA,
            pltpu.SemaphoreType.DMA,
            pltpu.SemaphoreType.DMA,
        ],
        compiler_params=pltpu.CompilerParams(
            collective_id=0, has_side_effects=True, vmem_limit_bytes=40 * 1024 * 1024
        ),
    )(
        *[
            hold(x, pltpu.HBM)
            for x in (
                current, next_fields, first_weight.transpose(0, 2, 1),
                first_bias[None], second_weight, second_bias[None],
            )
        ]
    )
    return pl.pallas_call(
        functools.partial(give, chans),
        out_shape=(
            jax.ShapeDtypeStruct((hid, rows, wide), BF16),
            jax.ShapeDtypeStruct((chans, rows, wide), BF16),
        ),
        in_specs=[vmem, vmem, hbm],
        out_specs=(hbm, hbm),
        scratch_shapes=[pltpu.SMEM((chans,), jnp.int32), pltpu.SemaphoreType.DMA((3,))],
        compiler_params=pltpu.CompilerParams(vmem_limit_bytes=8 * 1024 * 1024),
    )(made, moved, hold(reader_slot, pltpu.HBM))


def solution(mesh):
    in_specs = (P(None, "lat", "lon"), P(("lat", "lon"), None, None), P(), P(), P(), P(), P())
    out_specs = (P(None, "lat", "lon"), P(None, "lat", "lon"))
    return jax.shard_map(body, mesh=mesh, in_specs=in_specs, out_specs=out_specs, check_vma=False)
```

profile of v0, /device:TPU:9, one launch (start us, length us, event | category | flops | bytes accessed | tf_op | source)
XLA Modules:
  0.0 28.2 jit_solution(7893275600776572366)
XLA Ops:
  0.6 25.8 %shard_map.86 = (bf16[256,32,128]{2,1,0:T(8,128)(2,1)S(1)}, bf16[96,32,128]{2,1,0:T(8,128)(2,1)S(1)}) custom-call(bf16[69,32,128]{2,1,0:T(8,128)(2,1)} %cur_in.1, bf16[3,256,512]{2,1,0:T(8,128)(2,1)} %nf.1, bf16[9,69,256]{2,1,0:T(8,128)(2,1)} %bitcast.3, f32[1,256]{1,0:T(1,128)} %bitcast.4, bf16[9,256,256]{2,1,0:T(8,128)(2,1)} %w2_in.1, f32[1,256]{1,0:T(1,128)} %bitcast.5), custom_call_target="tpu_custom_call" | custom-call | tf_op jit(solution)/shard_map/pallas_call | solution.py:377
  26.5 1.7 %shard_map.87 = (bf16[256,32,128]{2,1,0:T(8,128)(2,1)}, bf16[69,32,128]{2,1,0:T(8,128)(2,1)}) custom-call(bf16[256,32,128]{2,1,0:T(8,128)(2,1)S(1)} %get-tuple-element.4.feat_in, bf16[96,32,128]{2,1,0:T(8,128)(2,1)S(1)} %get-tuple-element.5.moved, s32[69]{0:T(128)} %slot_in.1), custom_call_target="tpu_custom_call" | custom-call | tf_op jit(solution)/shard_map/pallas_call | solution.py:432
where the time goes:
time: 28.3 us; the launch traced here: 28.2 us
  Pallas kernels  27.5 us (97%)
  between operations  0.64 us (2%)
    pallas_call x1, Pallas kernels, body(): pl.pallas_call(functools.partial(kernel, dims), out_shape=(jax.ShapeDtype...  25.8 us
    pallas_call x1, Pallas kernels, body(): pl.pallas_call(functools.partial(give, chans), out_shape=(jax.ShapeDtypeS...  1.69 us

commit v1 on v0

--- a/solution.py
+++ b/solution.py
@@ -11,6 +11,9 @@
 F32 = jnp.float32
 BF16 = jnp.bfloat16
 LANES = 128
+NEAR = 4
+OUTER = 0
+INNER = 6
 G1 = 4
 G2 = 8
 
@@ -21,7 +24,7 @@
 
 def kernel(
     dims, cur_in, nf, w1_in, b1_in, w2_in, b2_in, feat, moved,
-    cur, w1, w2, b1, b2, yf, xf, parts, turned, xs, cols, csend, hcol, rsend, rrecv, en, eh,
+    cur, w1, w2, b1, b2, yf, xf, parts, turned, xs, cols, csend, hcol, ksend, krecv, rsend, rrecv, en, eh,
     xn, acc1, hp, hs, acc2, w1s, w2s, stats,
     in_sem, st_send, st_recv, ha_send, ha_recv, mv_send, mv_recv, own_sem,
 ):
@@ -46,14 +49,22 @@
 
     barrier = pltpu.get_barrier_semaphore()
 
-    def greet(d, carry):
-        t = lax.rem(me + d, n)
-        pl.semaphore_signal(
-            barrier, inc=1, device_id=(t // n_lon, lax.rem(t, n_lon)), device_id_type=MESH
-        )
-        return carry
-
-    lax.fori_loop(1, n, greet, 0)
+    def everyone(act):
+        across = [lax.rem(lon + b, n_lon) for b in range(n_lon)]
+        for b in range(1, n_lon):
+            act((lat, across[b]))
+
+        def along(a, carry):
+            tl = lax.rem(lat + a, n_lat)
+            for b in range(n_lon):
+                act((tl, across[b]))
+            return carry
+
+        lax.fori_loop(1, n_lat, along, 0)
+
+    everyone(
+        lambda t: pl.semaphore_signal(barrier, inc=1, device_id=t, device_id_type=MESH)
+    )
 
     loads[0].wait()
     x = cur[...].astype(F32)
@@ -94,58 +105,73 @@
         cols[1, base : base + part] = jnp.concatenate([e0, e1, w0, blank], axis=1)
     for side in range(2):
         csend[side] = cols[side].astype(BF16)
+        ksend[2 * side] = cols[side, 0:2]
+        ksend[2 * side + 1] = cols[side, rows - 2 : rows]
 
     pl.semaphore_wait(barrier, n - 1)
 
-    def stat_copy(d):
-        t = lax.rem(me + d, n)
-        return pltpu.make_async_remote_copy(
-            src_ref=stats.at[me], dst_ref=stats.at[me],
-            send_sem=st_send, recv_sem=st_recv,
-            device_id=(t // n_lon, lax.rem(t, n_lon)), device_id_type=MESH,
-        )
-
-    def stat_start(d, carry):
-        stat_copy(d).start()
-        return carry
-
-
-    lax.fori_loop(1, n, stat_start, 0)
+    everyone(
+        lambda t: pltpu.make_async_remote_copy(
+            src_ref=stats.at[me], dst_ref=stats.at[me], send_sem=st_send, recv_sem=st_recv,
+            device_id=t, device_id_type=MESH,
+        ).start()
+    )
 
     north, south = lax.rem(lat + n_lat - 1, n_lat), lax.rem(lat + 1, n_lat)
     west, east = lax.rem(lon + n_lon - 1, n_lon), lax.rem(lon + 1, n_lon)
-    halos = [
-        (rsend.at[0], rrecv.at[1], (north, lon)),
-        (rsend.at[1], rrecv.at[0], (south, lon)),
-    ]
+    above, below = lat > 0, lat < n_lat - 1
+    halos = []
     for side, col_to in ((0, west), (1, east)):
         into = 1 - side
-        halos.append((csend.at[side], hcol.at[into, pl.ds(16, rows)], (lat, col_to)))
-        halos.append((csend.at[side, pl.ds(0, 16)], hcol.at[into, pl.ds(16 + rows, 16)], (north, col_to)))
-        halos.append((csend.at[side, pl.ds(rows - 16, 16)], hcol.at[into, pl.ds(0, 16)], (south, col_to)))
+        halos.append((csend.at[side], hcol.at[into], (lat, col_to), None, None))
+        halos.append((ksend.at[2 * side], krecv.at[2 * into + 1], (north, col_to), above, below))
+        halos.append((ksend.at[2 * side + 1], krecv.at[2 * into], (south, col_to), below, above))
+    halos.append((rsend.at[0], rrecv.at[1], (north, lon), above, below))
+    halos.append((rsend.at[1], rrecv.at[0], (south, lon), below, above))
     copies = [
-        pltpu.make_async_remote_copy(
-            src_ref=src, dst_ref=dst, send_sem=ha_send.at[i], recv_sem=ha_recv.at[i],
-            device_id=where, device_id_type=MESH,
+        (
+            pltpu.make_async_remote_copy(
+                src_ref=src, dst_ref=dst, send_sem=ha_send.at[i], recv_sem=ha_recv.at[i],
+                device_id=where, device_id_type=MESH,
+            ),
+            sends, gets,
         )
-        for i, (src, dst, where) in enumerate(halos)
+        for i, (src, dst, where, sends, gets) in enumerate(halos)
     ]
-    for copy in copies:
-        copy.start()
-
+
+    def each(act, which):
+        for entry in copies:
+            if entry[which] is None:
+                act(entry[0])
+            else:
+                pl.when(entry[which])(functools.partial(act, entry[0]))
+
+    each(lambda copy: copy.start(), 1)
 
     half = max(n_lon // 2, 1)
 
+    if n_lon % 2 == 0:
+        mine, place = lon // half, lax.rem(lon, half)
+        outer = jnp.where(mine == 0, place < half - half // 2, place >= half // 2)
+    else:
+        outer = lon < 0
+
+    once = (half - 1) * n_lat
+
     def field_start(i, carry):
-        j = i // n_lat
         if n_lon % 2 == 0:
-            mine = lon // half
-            far = (1 - mine) * half + j
-            near = mine * half + lax.rem(lax.rem(lon, half) + j - half + 1, half)
-            tn = jnp.where(j < half, far, near)
+            f = i - once
+            turned_f = jnp.where(f < NEAR, once + f, jnp.where(f < NEAR + once, f - NEAR, f))
+            f = jnp.where(outer | (mine == 0), f, turned_f)
+            f = jnp.where(f < 0, 0, f)
+            is_near, is_own = i < once, i >= (n_lon - 1) * n_lat
+            tn = jnp.where(is_near, mine * half + lax.rem(place + i // n_lat + 1, half), (1 - mine) * half + f // n_lat)
+            tn = jnp.where(is_own, lon, tn)
+            k = lax.rem(jnp.where(is_near | is_own, i, f), n_lat) + jnp.where(is_own, 1, 0)
         else:
+            j = i // n_lat
             tn = lax.rem(lon + 1 + j, n_lon)
-        k = lax.rem(i, n_lat) + jnp.where(j == n_lon - 1, 1, 0)
+            k = lax.rem(i, n_lat) + jnp.where(j == n_lon - 1, 1, 0)
         tl = lax.rem(lat + k, n_lat)
         pltpu.make_async_remote_copy(
             src_ref=nf.at[:, pl.ds(pl.multiple_of(tl * rows, rows), rows), pl.ds(pl.multiple_of(tn * wide, wide), wide)],
@@ -156,8 +182,8 @@
         return carry
 
 
-    cuts = [min(e, n - 1) for e in (0, 0, 4, 8)] + [n - 1]
-    lax.fori_loop(0, cuts[1], field_start, 0)
+    cut1 = jnp.where(outer, once + OUTER, once + INNER)
+    lax.fori_loop(0, cut1, field_start, 0)
     own = pltpu.make_async_copy(
         nf.at[:, pl.ds(pl.multiple_of(lat * rows, rows), rows), pl.ds(pl.multiple_of(lon * wide, wide), wide)],
         moved.at[pl.ds(me * slots, slots)],
@@ -177,7 +203,6 @@
 
     lax.fori_loop(0, rows, turn_row, 0, unroll=4)
 
-    lax.fori_loop(cuts[1], cuts[2], field_start, 0)
     for load in loads[1:]:
         load.wait()
     for a in range(3):
@@ -195,10 +220,8 @@
 
     lax.fori_loop(0, 9, turn_weight, 0)
 
-    lax.fori_loop(cuts[2], cuts[3], field_start, 0)
-    for copy in copies:
-        copy.wait_recv()
-    lax.fori_loop(cuts[3], cuts[4], field_start, 0)
+    each(lambda copy: copy.wait_recv(), 2)
+    lax.fori_loop(cut1, n - 1, field_start, 0)
     tall = rows + 4
     step = en.shape[1]
     for side, p in ((0, 0), (1, rows + 2)):
@@ -207,7 +230,7 @@
 
     lane = lax.broadcasted_iota(jnp.int32, (1, kq), 1)
     for side in range(2):
-        far = hcol[side].astype(F32)[14 : 14 + tall]
+        far = jnp.concatenate([krecv[2 * side], hcol[side].astype(F32), krecv[2 * side + 1]], axis=0)
         mine = jnp.concatenate(
             [
                 xs[p, (wide - 16 if side == 0 else 0) : (wide if side == 0 else 16), :].astype(F32)[(15 if side == 0 else 0) : (16 if side == 0 else 1)]
@@ -339,8 +362,7 @@
     pltpu.make_async_copy(others, others, mv_recv).wait()
     pltpu.make_async_copy(others, others, mv_send).wait()
     pltpu.make_async_copy(stats.at[pl.ds(0, n - 1)], stats.at[pl.ds(0, n - 1)], st_send).wait()
-    for copy in copies:
-        copy.wait_send()
+    each(lambda copy: copy.wait_send(), 1)
 
 
 def give(chans, feat_in, moved, slot_in, feat, tile, slot, sems):
@@ -350,11 +372,8 @@
     out.start()
     want.wait()
 
-    def take(c, carry):
+    for c in range(chans):
         pltpu.make_async_copy(moved.at[slot[c]], tile.at[c], sems.at[2]).start()
-        return carry
-
-    lax.fori_loop(0, chans, take, 0)
     pltpu.make_async_copy(moved.at[pl.ds(0, chans)], tile, sems.at[2]).wait()
     out.wait()
 
@@ -395,7 +414,9 @@
             pltpu.VMEM((rows + 4, wide, kq), BF16),
             pltpu.VMEM((2, rows, kq), F32),
             pltpu.VMEM((2, rows, kq), BF16),
-            pltpu.VMEM((2, rows + 32, kq), BF16),
+            pltpu.VMEM((2, rows, kq), BF16),
+            pltpu.VMEM((4, 2, kq), F32),
+            pltpu.VMEM((4, 2, kq), F32),
             pltpu.VMEM((2, 2, cb, wide), BF16),
             pltpu.VMEM((2, 2, cb, wide), BF16),
             pltpu.VMEM((4, step, kq), F32),

time: 28.3 us -> 27.4 us (0.968); the launches traced: 28.2 us -> 26.9 us
  Pallas kernels: 27.5 us -> 26.3 us
    pallas_call x1, Pallas kernels: 25.8 us -> 24.7 us  [body(): pl.pallas_call(functools.partial(kernel, dims), out_shape=(jax.ShapeDtype...]
where the time goes in v1:
time: 27.4 us; the launch traced here: 26.9 us
  Pallas kernels  26.3 us (96%)
  between operations  0.64 us (2%)
    pallas_call x1, Pallas kernels, body(): pl.pallas_call(functools.partial(kernel, dims), out_shape=(jax.ShapeDtype...  24.7 us
    pallas_call x1, Pallas kernels, body(): pl.pallas_call(functools.partial(give, chans), out_shape=(jax.ShapeDtypeS...  1.57 us

profile of v1, /device:TPU:9, one launch (start us, length us, event | category | flops | bytes accessed | tf_op | source)
XLA Modules:
  0.0 26.9 jit_solution(2042623481846028130)
XLA Ops:
  0.6 24.7 %shard_map.86 = (bf16[256,32,128]{2,1,0:T(8,128)(2,1)S(1)}, bf16[96,32,128]{2,1,0:T(8,128)(2,1)S(1)}) custom-call(bf16[69,32,128]{2,1,0:T(8,128)(2,1)} %cur_in.1, bf16[3,256,512]{2,1,0:T(8,128)(2,1)} %nf.1, bf16[9,69,256]{2,1,0:T(8,128)(2,1)} %bitcast.3, f32[1,256]{1,0:T(1,128)} %bitcast.4, bf16[9,256,256]{2,1,0:T(8,128)(2,1)} %w2_in.1, f32[1,256]{1,0:T(1,128)} %bitcast.5), custom_call_target="tpu_custom_call" | custom-call | tf_op jit(solution)/shard_map/pallas_call | solution.py:396
  25.3 1.6 %shard_map.87 = (bf16[256,32,128]{2,1,0:T(8,128)(2,1)}, bf16[69,32,128]{2,1,0:T(8,128)(2,1)}) custom-call(bf16[256,32,128]{2,1,0:T(8,128)(2,1)S(1)} %get-tuple-element.4.feat_in, bf16[96,32,128]{2,1,0:T(8,128)(2,1)S(1)} %get-tuple-element.5.moved, s32[69]{0:T(128)} %slot_in.1), custom_call_target="tpu_custom_call" | custom-call | tf_op jit(solution)/shard_map/pallas_call | solution.py:453

commit v2 on v1

--- a/solution.py
+++ b/solution.py
@@ -11,6 +11,7 @@
 F32 = jnp.float32
 BF16 = jnp.bfloat16
 LANES = 128
+PIECES = 2
 NEAR = 4
 OUTER = 0
 INNER = 6
@@ -183,7 +184,8 @@
 
 
     cut1 = jnp.where(outer, once + OUTER, once + INNER)
-    lax.fori_loop(0, cut1, field_start, 0)
+    lax.fori_loop(once, cut1, field_start, 0)
+    lax.fori_loop(0, once, field_start, 0)
     own = pltpu.make_async_copy(
         nf.at[:, pl.ds(pl.multiple_of(lat * rows, rows), rows), pl.ds(pl.multiple_of(lon * wide, wide), wide)],
         moved.at[pl.ds(me * slots, slots)],
@@ -368,14 +370,16 @@
 def give(chans, feat_in, moved, slot_in, feat, tile, slot, sems):
     want = pltpu.make_async_copy(slot_in, slot, sems.at[0])
     want.start()
-    out = pltpu.make_async_copy(feat_in, feat, sems.at[1])
-    out.start()
+    part = feat.shape[0] // PIECES
+    for k in range(PIECES):
+        piece = pl.ds(k * part, part)
+        pltpu.make_async_copy(feat_in.at[piece], feat.at[piece], sems.at[1]).start()
     want.wait()
 
     for c in range(chans):
         pltpu.make_async_copy(moved.at[slot[c]], tile.at[c], sems.at[2]).start()
     pltpu.make_async_copy(moved.at[pl.ds(0, chans)], tile, sems.at[2]).wait()
-    out.wait()
+    pltpu.make_async_copy(feat_in, feat, sems.at[1]).wait()
 
 
 def body(current, next_fields, reader_slot, first_weight, first_bias, second_weight, second_bias):

time: 27.4 us -> 27.4 us (level)
  no operation moved by 1% of the time
where the time goes in v2:
time: 27.4 us; the launch traced here: 27.1 us
  Pallas kernels  26.4 us (96%)
  between operations  0.64 us (2%)
    pallas_call x1, Pallas kernels, body(): pl.pallas_call(functools.partial(kernel, dims), out_shape=(jax.ShapeDtype...  24.9 us
    pallas_call x1, Pallas kernels, body(): pl.pallas_call(functools.partial(give, chans), out_shape=(jax.ShapeDtypeS...  1.57 us

profile of v2, /device:TPU:9, one launch (start us, length us, event | category | flops | bytes accessed | tf_op | source)
XLA Modules:
  0.0 27.1 jit_solution(10399421544925725881)
XLA Ops:
  0.6 24.9 %shard_map.86 = (bf16[256,32,128]{2,1,0:T(8,128)(2,1)S(1)}, bf16[96,32,128]{2,1,0:T(8,128)(2,1)S(1)}) custom-call(bf16[69,32,128]{2,1,0:T(8,128)(2,1)} %cur_in.1, bf16[3,256,512]{2,1,0:T(8,128)(2,1)} %nf.1, bf16[9,69,256]{2,1,0:T(8,128)(2,1)} %bitcast.3, f32[1,256]{1,0:T(1,128)} %bitcast.4, bf16[9,256,256]{2,1,0:T(8,128)(2,1)} %w2_in.1, f32[1,256]{1,0:T(1,128)} %bitcast.5), custom_call_target="tpu_custom_call" | custom-call | tf_op jit(solution)/shard_map/pallas_call | solution.py:400
  25.5 1.6 %shard_map.87 = (bf16[256,32,128]{2,1,0:T(8,128)(2,1)}, bf16[69,32,128]{2,1,0:T(8,128)(2,1)}) custom-call(bf16[256,32,128]{2,1,0:T(8,128)(2,1)S(1)} %get-tuple-element.4.feat_in, bf16[96,32,128]{2,1,0:T(8,128)(2,1)S(1)} %get-tuple-element.5.moved, s32[69]{0:T(128)} %slot_in.1), custom_call_target="tpu_custom_call" | custom-call | tf_op jit(solution)/shard_map/pallas_call | solution.py:457
